TPU v7x, 32 devices: a whole 2x2x4 slice. The times are simulated.
32 devices in a mesh: dp: 2 (over core), tensor: 16 (over z, y, x).
Axes of the slice: x: 2, y: 2, z: 4, core: 2. Of those that a mesh axis runs over, the one named last changes fastest.
Arguments:
- inputs: bfloat16 [768, 6144], P(('dp', 'tensor')), may hold values from -0.29882812 to 0.29882812
- norm_gain: float32 [6144], replicated, may hold values from 0.1 to 1.9
- norm_bias: float32 [6144], replicated, may hold values from -3 to 3
- query_grad: bfloat16 [768, 12288], P('dp', 'tensor'), may hold values from -0.119628906 to 0.119628906
- stream_grad: bfloat16 [768, 6144], P(('dp', 'tensor')), may hold values from -2.390625 to 2.390625
- query_weight: bfloat16 [6144, 12288], P(None, 'tensor'), may hold values from -0.0546875 to 0.0546875
Outputs:
- input_grad: bfloat16 [768, 6144], P(('dp', 'tensor'))
- weight_grad: bfloat16 [6144, 12288], P(None, 'tensor')
All inputs are finite; a program needn't handle non-finite values.
Results may differ from a plain program's by a relative error of at most 0.019.
Values may be sent and summed in bfloat16 or wider, within the bound.
No kernel may reach another device: no remote copies, remote signals or barrier semaphores. Data moves between devices by JAX's collectives and lax.ppermute only.
A program may use at most 128 MiB of HBM per device.

v0:
```python
import jax
import jax.numpy as jnp
from jax import lax
from jax.experimental import pallas as pl
from jax.sharding import PartitionSpec as P


epsilon = 1e-05


def sizes_of(count):
    outer = 4 if count % 4 == 0 else 1
    rest = count // outer
    inner = 2 if rest % 2 == 0 else 1
    return (outer, rest // inner, inner)


def moved(sizes, axis, step):
    outer, middle, inner = sizes
    pairs = []
    for index in range(outer * middle * inner):
        place = [index // (middle * inner), index // inner % middle, index % inner]
        place[axis] = (place[axis] + step) % sizes[axis]
        pairs.append((index, (place[0] * middle + place[1]) * inner + place[2]))
    return pairs


def gather_pieces(sizes, axis, values):
    return [values] + [
        lax.ppermute(values, "tensor", moved(sizes, axis, -step)) for step in range(1, sizes[axis])
    ]


def row_selector(sizes, order, rows):
    index = lax.axis_index("tensor")
    outer, middle, inner = sizes
    own = [index // (middle * inner), index // inner % middle, index % inner]
    count = outer * middle * inner
    tokens = rows // count
    row = lax.broadcasted_iota(jnp.int32, (rows, rows), 0)
    column = lax.broadcasted_iota(jnp.int32, (rows, rows), 1)
    left = row // tokens
    places = [None, None, None]
    for axis in reversed(order):
        places[axis] = (left % sizes[axis] + own[axis]) % sizes[axis]
        left = left // sizes[axis]
    source = ((places[0] * middle + places[1]) * inner + places[2]) * tokens + row % tokens
    return (source == column).astype(jnp.bfloat16)


def picked(selector, values):
    return lax.dot_general(
        selector, values, (((1,), (0,)), ((), ())), preferred_element_type=jnp.float32
    ).astype(jnp.bfloat16)


def weight_kernel(counts, steps_each):
    def body(*refs):
        out_ref = refs[-1]
        step = pl.program_id(0)
        start = 0
        for number, count in enumerate(counts):
            piece_refs = refs[start : start + count]
            grad_ref = refs[start + count]
            start += count + 1

            @pl.when(step // steps_each == number)
            def _():
                tall = jnp.concatenate([ref[...] for ref in piece_refs], axis=0)
                out_ref[...] = lax.dot_general(
                    tall, grad_ref[...], (((0,), (0,)), ((), ())), preferred_element_type=jnp.float32
                ).astype(out_ref.dtype)

    return body


def weight_product(segments, grads, firsts, height, base):
    width = segments[0][0].shape[1]
    block = next(size for size in (512, 256, 128) if width % size == 0)
    steps_each = width // block
    features = grads[0].shape[1]
    places = [first // block for first in firsts]
    specs, operands = [], []
    for number, (pieces, grad) in enumerate(zip(segments, grads)):
        for piece in pieces:
            specs.append(
                pl.BlockSpec(
                    (piece.shape[0], block),
                    lambda i, n=number: (0, jnp.clip(i - n * steps_each, 0, steps_each - 1)),
                )
            )
            operands.append(piece)
        specs.append(pl.BlockSpec(grad.shape, lambda i: (0, 0)))
        operands.append(grad)
    aliases = {}
    if base is not None:
        aliases = {len(operands): 0}
        specs.append(pl.BlockSpec(memory_space=pl.ANY))
        operands.append(base)
    rows = grads[0].shape[0]

    def out_at(i):
        return (jnp.where(i < steps_each, places[0] + i, places[1] + i - steps_each), 0)

    return pl.pallas_call(
        weight_kernel([len(pieces) for pieces in segments], steps_each),
        grid=(2 * steps_each,),
        in_specs=specs,
        out_specs=pl.BlockSpec((block, features), out_at),
        out_shape=jax.ShapeDtypeStruct((height, features), jnp.bfloat16),
        input_output_aliases=aliases,
        cost_estimate=pl.CostEstimate(
            flops=4 * rows * width * features, transcendentals=0, bytes_accessed=4 * width * features
        ),
        name="weight_product",
    )(*operands)


def after(value, *others):
    return lax.optimization_barrier((value,) + others)[0]


def normalize(values, norm_gain, norm_bias):
    as_float = values.astype(jnp.float32)
    centre = jnp.mean(as_float, axis=-1, keepdims=True)
    offsets = as_float - centre
    variance = jnp.mean(offsets * offsets, axis=-1, keepdims=True)
    inverse = lax.rsqrt(variance + epsilon)
    scaled = offsets * inverse
    normed = (scaled * norm_gain + norm_bias).astype(jnp.bfloat16)
    return (scaled, inverse, normed)


def norm_backward(scaled, inverse, normed_grad, norm_gain, stream_grad):
    weighted = normed_grad * norm_gain
    first_moment = jnp.mean(weighted, axis=-1, keepdims=True)
    second_moment = jnp.mean(weighted * scaled, axis=-1, keepdims=True)
    result = stream_grad.astype(jnp.float32) + inverse * (
        weighted - first_moment - scaled * second_moment
    )
    return result.astype(jnp.bfloat16)


def split(values, count):
    tall = values.shape[0] // count
    return [values[step * tall : (step + 1) * tall] for step in range(count)]


def sent(chunks, sizes, axis):
    return [
        lax.ppermute(chunks[step], "tensor", moved(sizes, axis, step))
        for step in range(1, sizes[axis])
    ]


def added(own, received):
    total = own.astype(jnp.float32)
    for values in received:
        total = total + values.astype(jnp.float32)
    return total


def contracted(grad, weight_rows):
    return lax.dot_general(
        grad, weight_rows, (((1,), (1,)), ((), ())), preferred_element_type=jnp.float32
    ).astype(jnp.bfloat16)


def program(sizes, groups):
    orders = ((2, 1, 0), (1, 2, 0))

    def layer(inputs, norm_gain, norm_bias, query_grad, stream_grad, query_weight):
        width = inputs.shape[1] // 2
        rows = query_grad.shape[0]
        paired = groups == 2
        swap = [(0, 1), (1, 0)]

        selectors = [row_selector(sizes, order, rows) for order in orders]
        grads = [picked(selector, query_grad) for selector in selectors]
        weights = [query_weight[:width], query_weight[width:]]

        tops = [split(grads[n], sizes[order[0]]) for n, order in enumerate(orders)]
        going = [[contracted(g, weights[n]) for g in tops[n][1:]] for n in range(2)]
        leaving = [sent([None] + going[n], sizes, order[0]) for n, order in enumerate(orders)]

        inputs = after(inputs, *going[0], *going[1])
        scaled, inverse, normed = normalize(inputs, norm_gain, norm_bias)
        normed = after(normed)
        outer_pieces = gather_pieces(sizes, 0, normed)
        top0, top1, query_grad = lax.optimization_barrier(
            (tops[0][0], tops[1][0], query_grad, normed)
        )[:3]
        kept = [contracted(top0, weights[0]), contracted(top1, weights[1])]
        if paired:
            other_grad = lax.ppermute(query_grad, "dp", swap)
            other = [picked(selector, other_grad) for selector in selectors]
            grads = [jnp.concatenate(pair, axis=0) for pair in zip(grads, other)]
        kept = list(lax.optimization_barrier((*kept, *grads))[:2])

        totals = [added(kept[n], leaving[n]).astype(jnp.bfloat16) for n in range(2)]
        chunks = [split(totals[n], sizes[order[1]]) for n, order in enumerate(orders)]
        received = [sent(chunks[n], sizes, order[1]) for n, order in enumerate(orders)]

        outer_pieces = list(lax.optimization_barrier((*outer_pieces, *totals))[: sizes[0]])
        held = [
            jnp.concatenate(
                [piece[:, number * width : (number + 1) * width] for piece in outer_pieces], axis=0
            )
            for number in range(2)
        ]
        second = [gather_pieces(sizes, order[1], held[n]) for n, order in enumerate(orders)]

        kept = [chunk[0] for chunk in chunks]
        kept = list(lax.optimization_barrier((*kept, *held))[:2])
        total = jnp.concatenate(
            [added(kept[n], received[n]).astype(jnp.bfloat16) for n in range(2)], axis=1
        )
        chunks = split(total, sizes[0])
        normed_grad = added(chunks[0], sent(chunks, sizes, 0))
        input_grad = norm_backward(scaled, inverse, normed_grad, norm_gain, stream_grad)

        parts = 2 if width % 256 == 0 else 1
        wide = width // parts
        flat = [piece for pieces in second for piece in pieces]
        flat = list(lax.optimization_barrier((*flat, total))[: len(flat)])
        second = [flat[: len(second[0])], flat[len(second[0]) :]]
        segments = []
        for part in range(parts):
            at = slice(part * wide, (part + 1) * wide)
            held = [jnp.concatenate([p[:, at] for p in pieces], axis=0) for pieces in second]
            segments.append(
                [gather_pieces(sizes, order[0], held[n]) for n, order in enumerate(orders)]
            )
        weight_grad = None
        for part in range(parts):
            pieces = segments[part]
            if weight_grad is not None:
                late = [piece for own in pieces for piece in own[1:]]
                late = lax.optimization_barrier((*late, weight_grad))
                weight_grad, late = late[-1], list(late[:-1])
                pieces = [[own[0]] + [late.pop(0) for _ in own[1:]] for own in pieces]
            if paired:
                pieces = [own + [lax.ppermute(p, "dp", swap) for p in own] for own in pieces]
            weight_grad = weight_product(
                pieces, grads, (part * wide, width + part * wide), 2 * width, weight_grad
            )
        if groups > 1 and not paired:
            weight_grad = lax.psum(weight_grad, "dp")
        return (input_grad, weight_grad)

    return layer


def solution(mesh):
    placed = (
        P(("dp", "tensor"), None),
        P(),
        P(),
        P("dp", "tensor"),
        P(("dp", "tensor"), None),
        P(None, "tensor"),
    )
    return jax.shard_map(
        program(sizes_of(mesh.shape["tensor"]), mesh.shape["dp"]),
        mesh=mesh,
        in_specs=placed,
        out_specs=(P(("dp", "tensor"), None), P(None, "tensor")),
        check_vma=False,
    )
```

profile of v0, /device:TPU:9, one launch (start us, length us, event | category | flops | bytes accessed | tf_op | source)
XLA Modules:
  0.0 134.4 jit_solution(9144554866606476775)
XLA Ops:
  0.8 3.0 %convolution_convert_fusion.2 = bf16[384,768]{1,0:T(8,128)(2,1)S(1)} fusion(bf16[384,768]{1,0:T(8,128)(2,1)} %param.9, s32[384]{0:T(512)S(1)} %get-tuple-element.67, s32[384]{0:T(512)S(1)} %get-tuple-element.68, s32[]{:T(128)S(6)} %select_n.119, s32[]{:T(128)S(6)} %select_n.115, pred[384]{0:T(512)(128)(4,1)S(1)} %get-tuple-element.71, ...), kind=kOutput, calls=%fused_computation.29 | convolution fusion | flops 240648192 | bytes 1186572 | tf_op jit(solution)/shard_map/dot_general | solution.py:52
  3.8 1.8 %convolution_convert_fusion.3 = bf16[384,768]{1,0:T(8,128)(2,1)S(1)} fusion(bf16[384,768]{1,0:T(8,128)(2,1)S(1)} %copy-done.18, s32[384]{0:T(512)S(1)} %get-tuple-element.67, s32[384]{0:T(512)S(1)} %get-tuple-element.68, s32[]{:T(128)S(6)} %select_n.119, s32[]{:T(128)S(6)} %select_n.115, pred[384]{0:T(512)(128)(4,1)S(1)} %get-tuple-element.71, ...), kind=kOutput, calls=%fused_computation.30 | convolution fusion | flops 240648192 | bytes 1186572 | tf_op jit(solution)/shard_map/dot_general | solution.py:52
  5.6 1.7 %fusion.8 = bf16[192,3072]{1,0:T(8,128)(2,1)S(1)} fusion(bf16[6144,768]{1,0:T(8,128)(2,1)S(1)} %bitcast.7, bf16[384,768]{1,0:T(8,128)(2,1)S(1)} %convolution_convert_fusion.3), kind=kOutput, calls=%fused_computation.8 | convolution fusion | flops 906559488 | bytes 6193152 | tf_op jit(solution)/shard_map/dot_general | solution.py:164
  7.3 1.7 %fusion.14 = bf16[192,3072]{1,0:T(8,128)(2,1)S(1)} fusion(bf16[6144,768]{1,0:T(8,128)(2,1)S(1)} %bitcast.7, bf16[384,768]{1,0:T(8,128)(2,1)S(1)} %convolution_convert_fusion.2), kind=kOutput, calls=%fused_computation.10 | convolution fusion | flops 906559488 | bytes 6193152 | tf_op jit(solution)/shard_map/dot_general | solution.py:164
  9.6 1.4 %collective-permute-start.5 = (bf16[24,6144]{1,0:T(8,128)(2,1)S(1)}, bf16[24,6144]{1,0:T(8,128)(2,1)S(1)}, u32[]{:S(2)}, u32[]{:S(2)}) collective-permute-start(bf16[24,6144]{1,0:T(8,128)(2,1)S(1)} %fusion.26), channel_id=1, source_target_pairs={{0,4},{1,5},{2,6},{3,7},{4,8},{5,9},{6,10},{7,11},{8,12},{9,13},{1... | collective-permute-start | bytes 884744 | tf_op jit(solution)/shard_map/ppermute | solution.py:30
  12.1 1.4 %collective-permute-start.3 = (bf16[24,6144]{1,0:T(8,128)(2,1)S(1)}, bf16[24,6144]{1,0:T(8,128)(2,1)S(1)}, u32[]{:S(2)}, u32[]{:S(2)}) collective-permute-start(bf16[24,6144]{1,0:T(8,128)(2,1)S(1)} %fusion.26), channel_id=1, source_target_pairs={{0,12},{1,13},{2,14},{3,15},{4,0},{5,1},{6,2},{7,3},{8,4},{9,5},{1... | collective-permute-start | bytes 884744 | tf_op jit(solution)/shard_map/ppermute | solution.py:30
  14.8 1.9 %collective-permute-start = (bf16[384,768]{1,0:T(8,128)(2,1)S(1)}, bf16[384,768]{1,0:T(8,128)(2,1)S(1)}, u32[]{:S(2)}, u32[]{:S(2)}) collective-permute-start(bf16[384,768]{1,0:T(8,128)(2,1)S(1)} %copy-done.18), channel_id=1, source_target_pairs={{0,16},{16,0},{1,17},{17,1},{2,18},{18,2},{3,19},{19,3},{4,20},{20... | collective-permute-start | bytes 1769480 | tf_op jit(solution)/shard_map/ppermute | solution.py:195
  16.6 1.7 %fusion.11 = bf16[192,3072]{1,0:T(8,128)(2,1)S(1)} fusion(bf16[192,768]{1,0:T(8,128)(2,1)S(1)} %slice.122, bf16[6144,768]{1,0:T(8,128)(2,1)S(1)} %bitcast.7), kind=kOutput, calls=%fused_computation.9 | convolution fusion | flops 906559488 | bytes 6193152 | tf_op jit(solution)/shard_map/dot_general | solution.py:164
  18.3 1.7 %fusion.17 = bf16[192,3072]{1,0:T(8,128)(2,1)S(1)} fusion(bf16[192,768]{1,0:T(8,128)(2,1)S(1)} %slice-done, bf16[6144,768]{1,0:T(8,128)(2,1)S(1)} %bitcast.7), kind=kOutput, calls=%fused_computation.11 | convolution fusion | flops 906559488 | bytes 6193152 | tf_op jit(solution)/shard_map/dot_general | solution.py:164
  21.3 1.7 %convolution_convert_fusion.1 = bf16[384,768]{1,0:T(8,128)(2,1)S(1)} fusion(bf16[384,768]{1,0:T(8,128)(2,1)S(1)} %collective-permute-done, s32[384]{0:T(512)S(1)} %get-tuple-element.67, s32[384]{0:T(512)S(1)} %get-tuple-element.68, s32[]{:T(128)S(6)} %select_n.119, s32[]{:T(128)S(6)} %select_n.115, pred[384]{0:T(512)(128)(4,1)S(1)} %get-tuple-element.71, ...), kind=kOutput, calls=%fused_computation.28 | convolution fusion | flops 240648192 | bytes 1186572 | tf_op jit(solution)/shard_map/dot_general | solution.py:52
  24.2 1.8 %convolution_convert_fusion = bf16[384,768]{1,0:T(8,128)(2,1)S(1)} fusion(bf16[384,768]{1,0:T(8,128)(2,1)S(1)} %collective-permute-done, s32[384]{0:T(512)S(1)} %get-tuple-element.67, s32[384]{0:T(512)S(1)} %get-tuple-element.68, s32[]{:T(128)S(6)} %select_n.119, s32[]{:T(128)S(6)} %select_n.115, pred[384]{0:T(512)(128)(4,1)S(1)} %get-tuple-element.71, ...), kind=kOutput, calls=%fused_computation.27 | convolution fusion | flops 240648192 | bytes 1186572 | tf_op jit(solution)/shard_map/dot_general | solution.py:52
  27.1 12.4 %collective-permute-done.2 = bf16[192,3072]{1,0:T(8,128)(2,1)S(1)} collective-permute-done((bf16[192,3072]{1,0:T(8,128)(2,1)S(1)}, bf16[192,3072]{1,0:T(8,128)(2,1)S(1)}, u32[]{:S(2)}, u32[]{:S(2)}) %collective-permute-start.2) | collective-permute-done | bytes 1179680 | tf_op jit(solution)/shard_map/ppermute | solution.py:151
  41.2 6.3 %collective-permute-done.1 = bf16[192,3072]{1,0:T(8,128)(2,1)S(1)} collective-permute-done((bf16[192,3072]{1,0:T(8,128)(2,1)S(1)}, bf16[192,3072]{1,0:T(8,128)(2,1)S(1)}, u32[]{:S(2)}, u32[]{:S(2)}) %collective-permute-start.1) | collective-permute-done | bytes 1179680 | tf_op jit(solution)/shard_map/ppermute | solution.py:151
  48.5 1.3 collective-permute-start.12
  49.9 1.3 collective-permute-start.6
  51.2 10.6 %collective-permute-done.11 = bf16[96,3072]{1,0:T(8,128)(2,1)S(1)} collective-permute-done((bf16[96,3072]{1,0:T(8,128)(2,1)S(1)}, bf16[96,3072]{1,0:T(8,128)(2,1)S(1)}, u32[]{:S(2)}, u32[]{:S(2)}) %collective-permute-start.11) | collective-permute-done | bytes 589856 | tf_op jit(solution)/shard_map/ppermute | solution.py:30
  61.8 11.1 %collective-permute-done.12 = bf16[96,3072]{1,0:T(8,128)(2,1)S(1)} collective-permute-done((bf16[96,3072]{1,0:T(8,128)(2,1)S(1)}, bf16[96,3072]{1,0:T(8,128)(2,1)S(1)}, u32[]{:S(2)}, u32[]{:S(2)}) %collective-permute-start.12) | collective-permute-done | bytes 589856 | tf_op jit(solution)/shard_map/ppermute | solution.py:30
  76.1 3.1 %collective-permute-start.19 = (bf16[192,1536]{1,0:T(8,128)(2,1)S(1)}, bf16[192,1536]{1,0:T(8,128)(2,1)S(1)}, u32[]{:S(2)}, u32[]{:S(2)}) collective-permute-start(bf16[192,1536]{1,0:T(8,128)(2,1)S(1)} %pad_maximum_fusion.8.refs_5_), channel_id=1, source_target_pairs={{0,16},{16,0},{1,17},{17,1},{2,18},{18,2},{3,19},{19,3},{4,20},{20... | collective-permute-start | bytes 1769480 | tf_op jit(solution)/shard_map/ppermute | solution.py:243
  79.2 3.2 %collective-permute-start.9 = (bf16[24,6144]{1,0:T(8,128)(2,1)S(1)}, bf16[24,6144]{1,0:T(8,128)(2,1)S(1)}, u32[]{:S(2)}, u32[]{:S(2)}) collective-permute-start(bf16[24,6144]{1,0:T(8,128)(2,1)S(1)} %get-tuple-element.44), channel_id=1, source_target_pairs={{0,8},{1,9},{2,10},{3,11},{4,12},{5,13},{6,14},{7,15},{8,0},{9,1},... | collective-permute-start | bytes 884744 | tf_op jit(solution)/shard_map/ppermute | solution.py:151
  83.6 17.1 %collective-permute-done.9 = bf16[24,6144]{1,0:T(8,128)(2,1)S(1)} collective-permute-done((bf16[24,6144]{1,0:T(8,128)(2,1)S(1)}, bf16[24,6144]{1,0:T(8,128)(2,1)S(1)}, u32[]{:S(2)}, u32[]{:S(2)}) %collective-permute-start.9) | collective-permute-done | bytes 294944 | tf_op jit(solution)/shard_map/ppermute | solution.py:151
  101.3 3.1 %collective-permute-done.10 = bf16[24,6144]{1,0:T(8,128)(2,1)S(1)} collective-permute-done((bf16[24,6144]{1,0:T(8,128)(2,1)S(1)}, bf16[24,6144]{1,0:T(8,128)(2,1)S(1)}, u32[]{:S(2)}, u32[]{:S(2)}) %collective-permute-start.10) | collective-permute-done | bytes 294944 | tf_op jit(solution)/shard_map/ppermute | solution.py:151
  108.9 9.7 %weight_product.2.refs_10_ = bf16[6144,768]{1,0:T(8,128)(2,1)} custom-call(bf16[192,1536]{1,0:T(8,128)(2,1)} %copy-done.4, bf16[192,1536]{1,0:T(8,128)(2,1)} %copy-done.8, bf16[192,1536]{1,0:T(8,128)(2,1)} %copy-done.11, bf16[192,1536]{1,0:T(8,128)(2,1)} %collective-permute-done.17.refs_3_, bf16[768,768]{1,0:T(8,128)(2,1)} %pad_maximum_fusion.1.refs_4_, ...), custom_call_target="tpu_custom_call" | custom-call | flops 3623878656 | bytes 4718592 | tf_op jit(solution)/shard_map/weight_product/pallas_call | solution.py:105
  118.9 2.1 %collective-permute-done.13.refs_1_ = bf16[192,1536]{1,0:T(8,128)(2,1)S(1)} collective-permute-done((bf16[192,1536]{1,0:T(8,128)(2,1)S(1)}, bf16[192,1536]{1,0:T(8,128)(2,1)S(1)}, u32[]{:S(2)}, u32[]{:S(2)}) %collective-permute-start.13) | collective-permute-done | bytes 589856 | tf_op jit(solution)/shard_map/ppermute | solution.py:30
  124.7 9.7 %weight_product.3 = bf16[6144,768]{1,0:T(8,128)(2,1)} custom-call(bf16[192,1536]{1,0:T(8,128)(2,1)} %copy-done.2, bf16[192,1536]{1,0:T(8,128)(2,1)} %copy-done.10, bf16[192,1536]{1,0:T(8,128)(2,1)} %collective-permute-done.21.refs_2_, bf16[192,1536]{1,0:T(8,128)(2,1)} %copy-done.14, ...), custom_call_target="tpu_custom_call", output_to_operand_aliasing={{}: (10, {})} | custom-call | flops 3623878656 | bytes 4718592 | tf_op jit(solution)/shard_map/weight_product/pallas_call | solution.py:105
  (119 shorter events, 22.7 us)
Async XLA Ops:
  9.6 38.3 %collective-permute-start.5 = (bf16[24,6144]{1,0:T(8,128)(2,1)S(1)}, bf16[24,6144]{1,0:T(8,128)(2,1)S(1)}, u32[]{:S(2)}, u32[]{:S(2)}) collective-permute-start(bf16[24,6144]{1,0:T(8,128)(2,1)S(1)} %fusion.26), channel_id=1, source_target_pairs={{0,4},{1,5},{2,6},{3,7},{4,8},{5,9},{6,10},{7,11},{8,12},{9,13},{1... | collective-permute-start | bytes 884744 | tf_op jit(solution)/shard_map/ppermute | solution.py:30
  11.0 37.0 %collective-permute-start.4 = (bf16[24,6144]{1,0:T(8,128)(2,1)S(1)}, bf16[24,6144]{1,0:T(8,128)(2,1)S(1)}, u32[]{:S(2)}, u32[]{:S(2)}) collective-permute-start(bf16[24,6144]{1,0:T(8,128)(2,1)S(1)} %fusion.26), channel_id=1, source_target_pairs={{0,8},{1,9},{2,10},{3,11},{4,12},{5,13},{6,14},{7,15},{8,0},{9,1},... | collective-permute-start | bytes 884744 | tf_op jit(solution)/shard_map/ppermute | solution.py:30
  12.1 35.9 %collective-permute-start.3 = (bf16[24,6144]{1,0:T(8,128)(2,1)S(1)}, bf16[24,6144]{1,0:T(8,128)(2,1)S(1)}, u32[]{:S(2)}, u32[]{:S(2)}) collective-permute-start(bf16[24,6144]{1,0:T(8,128)(2,1)S(1)} %fusion.26), channel_id=1, source_target_pairs={{0,12},{1,13},{2,14},{3,15},{4,0},{5,1},{6,2},{7,3},{8,4},{9,5},{1... | collective-permute-start | bytes 884744 | tf_op jit(solution)/shard_map/ppermute | solution.py:30
  13.5 26.0 %collective-permute-start.2 = (bf16[192,3072]{1,0:T(8,128)(2,1)S(1)}, bf16[192,3072]{1,0:T(8,128)(2,1)S(1)}, u32[]{:S(2)}, u32[]{:S(2)}) collective-permute-start(bf16[192,3072]{1,0:T(8,128)(2,1)S(1)} %fusion.14), channel_id=1, source_target_pairs={{0,2},{1,3},{2,0},{3,1},{4,6},{5,7},{6,4},{7,5},{8,10},{9,11},{10,... | collective-permute-start | bytes 3538952 | tf_op jit(solution)/shard_map/ppermute | solution.py:151
  14.8 5.2 %collective-permute-start = (bf16[384,768]{1,0:T(8,128)(2,1)S(1)}, bf16[384,768]{1,0:T(8,128)(2,1)S(1)}, u32[]{:S(2)}, u32[]{:S(2)}) collective-permute-start(bf16[384,768]{1,0:T(8,128)(2,1)S(1)} %copy-done.18), channel_id=1, source_target_pairs={{0,16},{16,0},{1,17},{17,1},{2,18},{18,2},{3,19},{19,3},{4,20},{20... | collective-permute-start | bytes 1769480 | tf_op jit(solution)/shard_map/ppermute | solution.py:195
  20.0 27.6 %collective-permute-start.1 = (bf16[192,3072]{1,0:T(8,128)(2,1)S(1)}, bf16[192,3072]{1,0:T(8,128)(2,1)S(1)}, u32[]{:S(2)}, u32[]{:S(2)}) collective-permute-start(bf16[192,3072]{1,0:T(8,128)(2,1)S(1)} %fusion.8), channel_id=1, source_target_pairs={{0,1},{1,0},{2,3},{3,2},{4,5},{5,4},{6,7},{7,6},{8,9},{9,8},{10,11... | collective-permute-start | bytes 3538952 | tf_op jit(solution)/shard_map/ppermute | solution.py:151
  40.0 33.4 %collective-permute-start.7 = (bf16[96,3072]{1,0:T(8,128)(2,1)S(1)}, bf16[96,3072]{1,0:T(8,128)(2,1)S(1)}, u32[]{:S(2)}, u32[]{:S(2)}) collective-permute-start(bf16[96,3072]{1,0:T(8,128)(2,1)S(1)} %get-tuple-element.46), channel_id=1, source_target_pairs={{0,1},{1,0},{2,3},{3,2},{4,5},{5,4},{6,7},{7,6},{8,9},{9,8},{10,11... | collective-permute-start | bytes 1769480 | tf_op jit(solution)/shard_map/ppermute | solution.py:151
  48.2 13.6 %collective-permute-start.11 = (bf16[96,3072]{1,0:T(8,128)(2,1)S(1)}, bf16[96,3072]{1,0:T(8,128)(2,1)S(1)}, u32[]{:S(2)}, u32[]{:S(2)}) collective-permute-start(bf16[96,3072]{1,0:T(8,128)(2,1)S(1)} %pad_maximum_fusion.3), channel_id=1, source_target_pairs={{0,2},{1,3},{2,0},{3,1},{4,6},{5,7},{6,4},{7,5},{8,10},{9,11},{10,... | collective-permute-start | bytes 1769480 | tf_op jit(solution)/shard_map/ppermute | solution.py:30
  48.5 24.4 %collective-permute-start.12 = (bf16[96,3072]{1,0:T(8,128)(2,1)S(1)}, bf16[96,3072]{1,0:T(8,128)(2,1)S(1)}, u32[]{:S(2)}, u32[]{:S(2)}) collective-permute-start(bf16[96,3072]{1,0:T(8,128)(2,1)S(1)} %pad_maximum_fusion.4), channel_id=1, source_target_pairs={{0,1},{1,0},{2,3},{3,2},{4,5},{5,4},{6,7},{7,6},{8,9},{9,8},{10,11... | collective-permute-start | bytes 1769480 | tf_op jit(solution)/shard_map/ppermute | solution.py:30
  49.9 24.6 %collective-permute-start.6 = (bf16[96,3072]{1,0:T(8,128)(2,1)S(1)}, bf16[96,3072]{1,0:T(8,128)(2,1)S(1)}, u32[]{:S(2)}, u32[]{:S(2)}) collective-permute-start(bf16[96,3072]{1,0:T(8,128)(2,1)S(1)} %get-tuple-element.49), channel_id=1, source_target_pairs={{0,2},{1,3},{2,0},{3,1},{4,6},{5,7},{6,4},{7,5},{8,10},{9,11},{10,... | collective-permute-start | bytes 1769480 | tf_op jit(solution)/shard_map/ppermute | solution.py:151
  73.0 31.7 %collective-permute-start.18 = (bf16[192,1536]{1,0:T(8,128)(2,1)S(1)}, bf16[192,1536]{1,0:T(8,128)(2,1)S(1)}, u32[]{:S(2)}, u32[]{:S(2)}) collective-permute-start(bf16[192,1536]{1,0:T(8,128)(2,1)S(1)} %pad_maximum_fusion.8.refs_5_), channel_id=1, source_target_pairs={{0,2},{1,3},{2,0},{3,1},{4,6},{5,7},{6,4},{7,5},{8,10},{9,11},{10,... | collective-permute-start | bytes 1769480 | tf_op jit(solution)/shard_map/ppermute | solution.py:30
  74.7 7.7 %collective-permute-start.8 = (bf16[24,6144]{1,0:T(8,128)(2,1)S(1)}, bf16[24,6144]{1,0:T(8,128)(2,1)S(1)}, u32[]{:S(2)}, u32[]{:S(2)}) collective-permute-start(bf16[24,6144]{1,0:T(8,128)(2,1)S(1)} %get-tuple-element.43), channel_id=1, source_target_pairs={{0,4},{1,5},{2,6},{3,7},{4,8},{5,9},{6,10},{7,11},{8,12},{9,13},{1... | collective-permute-start | bytes 884744 | tf_op jit(solution)/shard_map/ppermute | solution.py:151
  74.8 30.7 %collective-permute-start.15 = (bf16[192,1536]{1,0:T(8,128)(2,1)S(1)}, bf16[192,1536]{1,0:T(8,128)(2,1)S(1)}, u32[]{:S(2)}, u32[]{:S(2)}) collective-permute-start(bf16[192,1536]{1,0:T(8,128)(2,1)S(1)} %pad_maximum_fusion.7.refs_0_), channel_id=1, source_target_pairs={{0,1},{1,0},{2,3},{3,2},{4,5},{5,4},{6,7},{7,6},{8,9},{9,8},{10,11... | collective-permute-start | bytes 1769480 | tf_op jit(solution)/shard_map/ppermute | solution.py:30
  76.1 30.3 %collective-permute-start.19 = (bf16[192,1536]{1,0:T(8,128)(2,1)S(1)}, bf16[192,1536]{1,0:T(8,128)(2,1)S(1)}, u32[]{:S(2)}, u32[]{:S(2)}) collective-permute-start(bf16[192,1536]{1,0:T(8,128)(2,1)S(1)} %pad_maximum_fusion.8.refs_5_), channel_id=1, source_target_pairs={{0,16},{16,0},{1,17},{17,1},{2,18},{18,2},{3,19},{19,3},{4,20},{20... | collective-permute-start | bytes 1769480 | tf_op jit(solution)/shard_map/ppermute | solution.py:243
  79.2 21.5 %collective-permute-start.9 = (bf16[24,6144]{1,0:T(8,128)(2,1)S(1)}, bf16[24,6144]{1,0:T(8,128)(2,1)S(1)}, u32[]{:S(2)}, u32[]{:S(2)}) collective-permute-start(bf16[24,6144]{1,0:T(8,128)(2,1)S(1)} %get-tuple-element.44), channel_id=1, source_target_pairs={{0,8},{1,9},{2,10},{3,11},{4,12},{5,13},{6,14},{7,15},{8,0},{9,1},... | collective-permute-start | bytes 884744 | tf_op jit(solution)/shard_map/ppermute | solution.py:151
  82.4 22.0 %collective-permute-start.10 = (bf16[24,6144]{1,0:T(8,128)(2,1)S(1)}, bf16[24,6144]{1,0:T(8,128)(2,1)S(1)}, u32[]{:S(2)}, u32[]{:S(2)}) collective-permute-start(bf16[24,6144]{1,0:T(8,128)(2,1)S(1)} %get-tuple-element.45), channel_id=1, source_target_pairs={{0,12},{1,13},{2,14},{3,15},{4,0},{5,1},{6,2},{7,3},{8,4},{9,5},{1... | collective-permute-start | bytes 884744 | tf_op jit(solution)/shard_map/ppermute | solution.py:151
  100.7 6.9 %collective-permute-start.16 = (bf16[192,1536]{1,0:T(8,128)(2,1)S(1)}, bf16[192,1536]{1,0:T(8,128)(2,1)S(1)}, u32[]{:S(2)}, u32[]{:S(2)}) collective-permute-start(bf16[192,1536]{1,0:T(8,128)(2,1)S(1)} %pad_maximum_fusion.7.refs_0_), channel_id=1, source_target_pairs={{0,16},{16,0},{1,17},{17,1},{2,18},{18,2},{3,19},{19,3},{4,20},{20... | collective-permute-start | bytes 1769480 | tf_op jit(solution)/shard_map/ppermute | solution.py:243
  104.4 14.6 %collective-permute-start.14 = (bf16[192,1536]{1,0:T(8,128)(2,1)S(1)}, bf16[192,1536]{1,0:T(8,128)(2,1)}, u32[]{:S(2)}, u32[]{:S(2)}) collective-permute-start(bf16[192,1536]{1,0:T(8,128)(2,1)S(1)} %pad_maximum_fusion.6.refs_5_), channel_id=1, source_target_pairs={{0,2},{1,3},{2,0},{3,1},{4,6},{5,7},{6,4},{7,5},{8,10},{9,11},{10,... | collective-permute-start | bytes 1769480 | tf_op jit(solution)/shard_map/ppermute | solution.py:30
  104.8 3.4 %collective-permute-start.20 = (bf16[192,1536]{1,0:T(8,128)(2,1)S(1)}, bf16[192,1536]{1,0:T(8,128)(2,1)S(1)}, u32[]{:S(2)}, u32[]{:S(2)}) collective-permute-start(bf16[192,1536]{1,0:T(8,128)(2,1)S(1)} %collective-permute-done.18.refs_6_), channel_id=1, source_target_pairs={{0,16},{16,0},{1,17},{17,1},{2,18},{18,2},{3,19},{19,3},{4,20},{20... | collective-permute-start | bytes 1769480 | tf_op jit(solution)/shard_map/ppermute | solution.py:243
  105.5 3.5 %collective-permute-start.17 = (bf16[192,1536]{1,0:T(8,128)(2,1)S(1)}, bf16[192,1536]{1,0:T(8,128)(2,1)}, u32[]{:S(2)}, u32[]{:S(2)}) collective-permute-start(bf16[192,1536]{1,0:T(8,128)(2,1)S(1)} %collective-permute-done.15.refs_1_), channel_id=1, source_target_pairs={{0,16},{16,0},{1,17},{17,1},{2,18},{18,2},{3,19},{19,3},{4,20},{20... | collective-permute-start | bytes 1769480 | tf_op jit(solution)/shard_map/ppermute | solution.py:243
  106.3 14.7 %collective-permute-start.13 = (bf16[192,1536]{1,0:T(8,128)(2,1)S(1)}, bf16[192,1536]{1,0:T(8,128)(2,1)S(1)}, u32[]{:S(2)}, u32[]{:S(2)}) collective-permute-start(bf16[192,1536]{1,0:T(8,128)(2,1)S(1)} %pad_maximum_fusion.5.refs_0_), channel_id=1, source_target_pairs={{0,1},{1,0},{2,3},{3,2},{4,5},{5,4},{6,7},{7,6},{8,9},{9,8},{10,11... | collective-permute-start | bytes 1769480 | tf_op jit(solution)/shard_map/ppermute | solution.py:30
  107.6 15.5 %collective-permute-start.23 = (bf16[192,1536]{1,0:T(8,128)(2,1)S(1)}, bf16[192,1536]{1,0:T(8,128)(2,1)S(1)}, u32[]{:S(2)}, u32[]{:S(2)}) collective-permute-start(bf16[192,1536]{1,0:T(8,128)(2,1)S(1)} %pad_maximum_fusion.6.refs_5_), channel_id=1, source_target_pairs={{0,16},{16,0},{1,17},{17,1},{2,18},{18,2},{3,19},{19,3},{4,20},{20... | collective-permute-start | bytes 1769480 | tf_op jit(solution)/shard_map/ppermute | solution.py:243
  108.1 14.9 %collective-permute-start.21 = (bf16[192,1536]{1,0:T(8,128)(2,1)S(1)}, bf16[192,1536]{1,0:T(8,128)(2,1)}, u32[]{:S(2)}, u32[]{:S(2)}) collective-permute-start(bf16[192,1536]{1,0:T(8,128)(2,1)S(1)} %pad_maximum_fusion.5.refs_0_), channel_id=1, source_target_pairs={{0,16},{16,0},{1,17},{17,1},{2,18},{18,2},{3,19},{19,3},{4,20},{20... | collective-permute-start | bytes 1769480 | tf_op jit(solution)/shard_map/ppermute | solution.py:243
  121.0 2.7 %collective-permute-start.22 = (bf16[192,1536]{1,0:T(8,128)(2,1)S(1)}, bf16[192,1536]{1,0:T(8,128)(2,1)S(1)}, u32[]{:S(2)}, u32[]{:S(2)}) collective-permute-start(bf16[192,1536]{1,0:T(8,128)(2,1)S(1)} %collective-permute-done.13.refs_1_), channel_id=1, source_target_pairs={{0,16},{16,0},{1,17},{17,1},{2,18},{18,2},{3,19},{19,3},{4,20},{20... | collective-permute-start | bytes 1769480 | tf_op jit(solution)/shard_map/ppermute | solution.py:243
  (24 other events, 143.1 us)
where the time goes:
time: 135 us; the launch traced here: 134 us
  waiting for transfers between devices  64.6 us (48%)
  starting transfers between devices  26.1 us (19%)
  Pallas kernels  19.4 us (14%)
  matrix products  14.9 us (11%)
  other arithmetic  5.68 us (4%)
  local copies, waits for them, and re-layouts  2.43 us (2%)
    ppermute x7, waiting for transfers between devices, sent(): lax.ppermute(chunks[step], 'tensor', moved(sizes, axis, step))  39.8 us
    ppermute x9, waiting for transfers between devices, gather_pieces(): lax.ppermute(values, 'tensor', moved(sizes, axis, -step))  24 us
    pallas_call x2, Pallas kernels, weight_product(): pl.pallas_call(weight_kernel([len(pieces) for pieces in segments], steps_...  19.4 us
    ppermute x7, starting transfers between devices, sent(): lax.ppermute(chunks[step], 'tensor', moved(sizes, axis, step))  9.44 us
    ppermute x9, starting transfers between devices, gather_pieces(): lax.ppermute(values, 'tensor', moved(sizes, axis, -step))  8.53 us
    dot_general x4, matrix products, picked(): lax.dot_general(selector, values, (((1,), (0,)), ((), ())), preferred_ele...  8.23 us
    dot_general x4, matrix products, contracted(): lax.dot_general(grad, weight_rows, (((1,), (1,)), ((), ())), preferred_el...  6.7 us
    ppermute x8, starting transfers between devices, layer(): lax.ppermute(p, 'dp', swap)  6.24 us
  transfers between devices with their start and end apart: 25, of which 11 were waited for; matrix products, arithmetic and copies ran while one was open for 9% of the time, Pallas kernels for 7%

commit v1 on v0

--- a/solution.py
+++ b/solution.py
@@ -216,8 +216,7 @@
             [added(kept[n], received[n]).astype(jnp.bfloat16) for n in range(2)], axis=1
         )
         chunks = split(total, sizes[0])
-        normed_grad = added(chunks[0], sent(chunks, sizes, 0))
-        input_grad = norm_backward(scaled, inverse, normed_grad, norm_gain, stream_grad)
+        third = sent(chunks, sizes, 0)
 
         parts = 2 if width % 256 == 0 else 1
         wide = width // parts
@@ -236,14 +235,16 @@
             pieces = segments[part]
             if weight_grad is not None:
                 late = [piece for own in pieces for piece in own[1:]]
-                late = lax.optimization_barrier((*late, weight_grad))
-                weight_grad, late = late[-1], list(late[:-1])
+                late = lax.optimization_barrier((*late, *third, weight_grad))
+                weight_grad, third, late = late[-1], late[-sizes[0] : -1], list(late[: -sizes[0]])
                 pieces = [[own[0]] + [late.pop(0) for _ in own[1:]] for own in pieces]
             if paired:
                 pieces = [own + [lax.ppermute(p, "dp", swap) for p in own] for own in pieces]
             weight_grad = weight_product(
                 pieces, grads, (part * wide, width + part * wide), 2 * width, weight_grad
             )
+        normed_grad = added(chunks[0], third)
+        input_grad = norm_backward(scaled, inverse, normed_grad, norm_gain, stream_grad)
         if groups > 1 and not paired:
             weight_grad = lax.psum(weight_grad, "dp")
         return (input_grad, weight_grad)

time: 135 us -> 139 us (1.030)
  the two profiles are of different devices: /device:TPU:9 before, /device:TPU:0 now
where the time goes in v1:
time: 139 us
  waiting for transfers between devices  68.4 us (49%)
  starting transfers between devices  22.7 us (16%)
  Pallas kernels  19.4 us (14%)
  matrix products  14.9 us (11%)
  other arithmetic  7.73 us (6%)
  local copies, waits for them, and re-layouts  4.11 us (3%)
    ppermute x7, waiting for transfers between devices, sent(): lax.ppermute(chunks[step], 'tensor', moved(sizes, axis, step))  35.1 us
    ppermute x9, waiting for transfers between devices, gather_pieces(): lax.ppermute(values, 'tensor', moved(sizes, axis, -step))  32.6 us
    pallas_call x2, Pallas kernels, weight_product(): pl.pallas_call(weight_kernel([len(pieces) for pieces in segments], steps_...  19.4 us
    ppermute x9, starting transfers between devices, gather_pieces(): lax.ppermute(values, 'tensor', moved(sizes, axis, -step))  13.3 us
    ppermute x7, starting transfers between devices, sent(): lax.ppermute(chunks[step], 'tensor', moved(sizes, axis, step))  8.51 us
    dot_general x4, matrix products, picked(): lax.dot_general(selector, values, (((1,), (0,)), ((), ())), preferred_ele...  8.19 us
    dot_general x4, matrix products, contracted(): lax.dot_general(grad, weight_rows, (((1,), (1,)), ((), ())), preferred_el...  6.69 us
    unnamed x48, local copies, waits for them, and re-layouts  3.68 us
  transfers between devices with their start and end apart: 25, of which 10 were waited for; matrix products, arithmetic and copies ran while one was open for 10% of the time, Pallas kernels for 7%

profile of v1, /device:TPU:0, one launch (start us, length us, event | category | flops | bytes accessed | tf_op | source)
XLA Modules:
  0.0 138.5 jit_solution(4796993583874608090)
XLA Ops:
  0.8 3.0 %convolution_convert_fusion.2 = bf16[384,768]{1,0:T(8,128)(2,1)S(1)} fusion(bf16[384,768]{1,0:T(8,128)(2,1)} %param.9, s32[384]{0:T(512)S(1)} %get-tuple-element.73, s32[384]{0:T(512)S(1)} %get-tuple-element.74, s32[]{:T(128)S(6)} %select_n.119, s32[]{:T(128)S(6)} %select_n.115, pred[384]{0:T(512)(128)(4,1)S(1)} %get-tuple-element.77, ...), kind=kOutput, calls=%fused_computation.29 | convolution fusion | flops 240648192 | bytes 1186572 | tf_op jit(solution)/shard_map/dot_general | solution.py:52
  3.8 1.8 %convolution_convert_fusion.3 = bf16[384,768]{1,0:T(8,128)(2,1)S(1)} fusion(bf16[384,768]{1,0:T(8,128)(2,1)S(1)} %copy-done.20, s32[384]{0:T(512)S(1)} %get-tuple-element.73, s32[384]{0:T(512)S(1)} %get-tuple-element.74, s32[]{:T(128)S(6)} %select_n.119, s32[]{:T(128)S(6)} %select_n.115, pred[384]{0:T(512)(128)(4,1)S(1)} %get-tuple-element.77, ...), kind=kOutput, calls=%fused_computation.30 | convolution fusion | flops 240648192 | bytes 1186572 | tf_op jit(solution)/shard_map/dot_general | solution.py:52
  5.6 1.7 %fusion.8 = bf16[192,3072]{1,0:T(8,128)(2,1)S(1)} fusion(bf16[6144,768]{1,0:T(8,128)(2,1)S(1)} %bitcast.7, bf16[384,768]{1,0:T(8,128)(2,1)S(1)} %convolution_convert_fusion.3), kind=kOutput, calls=%fused_computation.8 | convolution fusion | flops 906559488 | bytes 6193152 | tf_op jit(solution)/shard_map/dot_general | solution.py:164
  7.3 1.7 %fusion.14 = bf16[192,3072]{1,0:T(8,128)(2,1)S(1)} fusion(bf16[6144,768]{1,0:T(8,128)(2,1)S(1)} %bitcast.7, bf16[384,768]{1,0:T(8,128)(2,1)S(1)} %convolution_convert_fusion.2), kind=kOutput, calls=%fused_computation.10 | convolution fusion | flops 906559488 | bytes 6193152 | tf_op jit(solution)/shard_map/dot_general | solution.py:164
  9.6 3.1 %collective-permute-start.5 = (bf16[24,6144]{1,0:T(8,128)(2,1)S(1)}, bf16[24,6144]{1,0:T(8,128)(2,1)S(1)}, u32[]{:S(2)}, u32[]{:S(2)}) collective-permute-start(bf16[24,6144]{1,0:T(8,128)(2,1)S(1)} %fusion.26), channel_id=1, source_target_pairs={{0,4},{1,5},{2,6},{3,7},{4,8},{5,9},{6,10},{7,11},{8,12},{9,13},{1... | collective-permute-start | bytes 884744 | tf_op jit(solution)/shard_map/ppermute | solution.py:30
  12.8 2.6 %collective-permute-start.4 = (bf16[24,6144]{1,0:T(8,128)(2,1)S(1)}, bf16[24,6144]{1,0:T(8,128)(2,1)S(1)}, u32[]{:S(2)}, u32[]{:S(2)}) collective-permute-start(bf16[24,6144]{1,0:T(8,128)(2,1)S(1)} %fusion.26), channel_id=1, source_target_pairs={{0,8},{1,9},{2,10},{3,11},{4,12},{5,13},{6,14},{7,15},{8,0},{9,1},... | collective-permute-start | bytes 884744 | tf_op jit(solution)/shard_map/ppermute | solution.py:30
  18.3 1.7 %fusion.11 = bf16[192,3072]{1,0:T(8,128)(2,1)S(1)} fusion(bf16[192,768]{1,0:T(8,128)(2,1)S(1)} %slice.122, bf16[6144,768]{1,0:T(8,128)(2,1)S(1)} %bitcast.7), kind=kOutput, calls=%fused_computation.9 | convolution fusion | flops 906559488 | bytes 6193152 | tf_op jit(solution)/shard_map/dot_general | solution.py:164
  20.0 1.7 %fusion.17 = bf16[192,3072]{1,0:T(8,128)(2,1)S(1)} fusion(bf16[192,768]{1,0:T(8,128)(2,1)S(1)} %slice-done, bf16[6144,768]{1,0:T(8,128)(2,1)S(1)} %bitcast.7), kind=kOutput, calls=%fused_computation.11 | convolution fusion | flops 906559488 | bytes 6193152 | tf_op jit(solution)/shard_map/dot_general | solution.py:164
  21.7 1.6 %collective-permute-start.1 = (bf16[192,3072]{1,0:T(8,128)(2,1)S(1)}, bf16[192,3072]{1,0:T(8,128)(2,1)S(1)}, u32[]{:S(2)}, u32[]{:S(2)}) collective-permute-start(bf16[192,3072]{1,0:T(8,128)(2,1)S(1)} %fusion.8), channel_id=1, source_target_pairs={{0,1},{1,0},{2,3},{3,2},{4,5},{5,4},{6,7},{7,6},{8,9},{9,8},{10,11... | collective-permute-start | bytes 3538952 | tf_op jit(solution)/shard_map/ppermute | solution.py:151
  23.3 1.7 %convolution_convert_fusion.1 = bf16[384,768]{1,0:T(8,128)(2,1)S(1)} fusion(bf16[384,768]{1,0:T(8,128)(2,1)S(1)} %collective-permute-done, s32[384]{0:T(512)S(1)} %get-tuple-element.73, s32[384]{0:T(512)S(1)} %get-tuple-element.74, s32[]{:T(128)S(6)} %select_n.119, s32[]{:T(128)S(6)} %select_n.115, pred[384]{0:T(512)(128)(4,1)S(1)} %get-tuple-element.77, ...), kind=kOutput, calls=%fused_computation.28 | convolution fusion | flops 240648192 | bytes 1186572 | tf_op jit(solution)/shard_map/dot_general | solution.py:52
  26.2 1.7 %convolution_convert_fusion = bf16[384,768]{1,0:T(8,128)(2,1)S(1)} fusion(bf16[384,768]{1,0:T(8,128)(2,1)S(1)} %collective-permute-done, s32[384]{0:T(512)S(1)} %get-tuple-element.73, s32[384]{0:T(512)S(1)} %get-tuple-element.74, s32[]{:T(128)S(6)} %select_n.119, s32[]{:T(128)S(6)} %select_n.115, pred[384]{0:T(512)(128)(4,1)S(1)} %get-tuple-element.77, ...), kind=kOutput, calls=%fused_computation.27 | convolution fusion | flops 240648192 | bytes 1186572 | tf_op jit(solution)/shard_map/dot_general | solution.py:52
  29.0 14.5 %collective-permute-done.2 = bf16[192,3072]{1,0:T(8,128)(2,1)S(1)} collective-permute-done((bf16[192,3072]{1,0:T(8,128)(2,1)S(1)}, bf16[192,3072]{1,0:T(8,128)(2,1)S(1)}, u32[]{:S(2)}, u32[]{:S(2)}) %collective-permute-start.2) | collective-permute-done | bytes 1179680 | tf_op jit(solution)/shard_map/ppermute | solution.py:151
  44.0 1.6 %collective-permute-start.7 = (bf16[96,3072]{1,0:T(8,128)(2,1)S(1)}, bf16[96,3072]{1,0:T(8,128)(2,1)S(1)}, u32[]{:S(2)}, u32[]{:S(2)}) collective-permute-start(bf16[96,3072]{1,0:T(8,128)(2,1)S(1)} %get-tuple-element.52), channel_id=1, source_target_pairs={{0,1},{1,0},{2,3},{3,2},{4,5},{5,4},{6,7},{7,6},{8,9},{9,8},{10,11... | collective-permute-start | bytes 1769480 | tf_op jit(solution)/shard_map/ppermute | solution.py:151
  45.6 5.0 %collective-permute-done.1 = bf16[192,3072]{1,0:T(8,128)(2,1)S(1)} collective-permute-done((bf16[192,3072]{1,0:T(8,128)(2,1)S(1)}, bf16[192,3072]{1,0:T(8,128)(2,1)S(1)}, u32[]{:S(2)}, u32[]{:S(2)}) %collective-permute-start.1) | collective-permute-done | bytes 1179680 | tf_op jit(solution)/shard_map/ppermute | solution.py:151
  51.8 1.6 %collective-permute-start.9 = (bf16[96,3072]{1,0:T(8,128)(2,1)S(1)}, bf16[96,3072]{1,0:T(8,128)(2,1)S(1)}, u32[]{:S(2)}, u32[]{:S(2)}) collective-permute-start(bf16[96,3072]{1,0:T(8,128)(2,1)S(1)} %pad_maximum_fusion.4), channel_id=1, source_target_pairs={{0,1},{1,0},{2,3},{3,2},{4,5},{5,4},{6,7},{7,6},{8,9},{9,8},{10,11... | collective-permute-start | bytes 1769480 | tf_op jit(solution)/shard_map/ppermute | solution.py:30
  53.5 1.6 %collective-permute-start.6 = (bf16[96,3072]{1,0:T(8,128)(2,1)S(1)}, bf16[96,3072]{1,0:T(8,128)(2,1)S(1)}, u32[]{:S(2)}, u32[]{:S(2)}) collective-permute-start(bf16[96,3072]{1,0:T(8,128)(2,1)S(1)} %get-tuple-element.55), channel_id=1, source_target_pairs={{0,2},{1,3},{2,0},{3,1},{4,6},{5,7},{6,4},{7,5},{8,10},{9,11},{10,... | collective-permute-start | bytes 1769480 | tf_op jit(solution)/shard_map/ppermute | solution.py:151
  55.1 12.4 %collective-permute-done.8 = bf16[96,3072]{1,0:T(8,128)(2,1)S(1)} collective-permute-done((bf16[96,3072]{1,0:T(8,128)(2,1)S(1)}, bf16[96,3072]{1,0:T(8,128)(2,1)S(1)}, u32[]{:S(2)}, u32[]{:S(2)}) %collective-permute-start.8) | collective-permute-done | bytes 589856 | tf_op jit(solution)/shard_map/ppermute | solution.py:30
  67.5 7.9 %collective-permute-done.9 = bf16[96,3072]{1,0:T(8,128)(2,1)S(1)} collective-permute-done((bf16[96,3072]{1,0:T(8,128)(2,1)S(1)}, bf16[96,3072]{1,0:T(8,128)(2,1)S(1)}, u32[]{:S(2)}, u32[]{:S(2)}) %collective-permute-start.9) | collective-permute-done | bytes 589856 | tf_op jit(solution)/shard_map/ppermute | solution.py:30
  81.2 10.7 %collective-permute-done.18.refs_6_ = bf16[192,1536]{1,0:T(8,128)(2,1)S(1)} collective-permute-done((bf16[192,1536]{1,0:T(8,128)(2,1)S(1)}, bf16[192,1536]{1,0:T(8,128)(2,1)S(1)}, u32[]{:S(2)}, u32[]{:S(2)}) %collective-permute-start.18) | collective-permute-done | bytes 589856 | tf_op jit(solution)/shard_map/ppermute | solution.py:30
  91.9 1.5 %collective-permute-done.15.refs_1_ = bf16[192,1536]{1,0:T(8,128)(2,1)S(1)} collective-permute-done((bf16[192,1536]{1,0:T(8,128)(2,1)S(1)}, bf16[192,1536]{1,0:T(8,128)(2,1)S(1)}, u32[]{:S(2)}, u32[]{:S(2)}) %collective-permute-start.15) | collective-permute-done | bytes 589856 | tf_op jit(solution)/shard_map/ppermute | solution.py:30
  98.0 9.7 %weight_product.2.refs_10_ = bf16[6144,768]{1,0:T(8,128)(2,1)} custom-call(bf16[192,1536]{1,0:T(8,128)(2,1)} %copy-done.4, bf16[192,1536]{1,0:T(8,128)(2,1)} %copy-done.10, bf16[192,1536]{1,0:T(8,128)(2,1)} %copy-done.9, bf16[192,1536]{1,0:T(8,128)(2,1)} %copy-done.14, bf16[768,768]{1,0:T(8,128)(2,1)} %pad_maximum_fusion.1.refs_4_, ...), custom_call_target="tpu_custom_call" | custom-call | flops 3623878656 | bytes 4718592 | tf_op jit(solution)/shard_map/weight_product/pallas_call | solution.py:105
  107.8 2.5 %collective-permute-done.14 = bf16[24,6144]{1,0:T(8,128)(2,1)S(1)} collective-permute-done((bf16[24,6144]{1,0:T(8,128)(2,1)}, bf16[24,6144]{1,0:T(8,128)(2,1)S(1)}, u32[]{:S(2)}, u32[]{:S(2)}) %collective-permute-start.14) | collective-permute-done | bytes 294944 | tf_op jit(solution)/shard_map/ppermute | solution.py:151
  111.0 12.3 %collective-permute-done.13 = bf16[24,6144]{1,0:T(8,128)(2,1)} collective-permute-done((bf16[24,6144]{1,0:T(8,128)(2,1)}, bf16[24,6144]{1,0:T(8,128)(2,1)}, u32[]{:S(2)}, u32[]{:S(2)}) %collective-permute-start.13) | collective-permute-done | bytes 294944 | tf_op jit(solution)/shard_map/ppermute | solution.py:151
  128.8 9.7 %weight_product.3 = bf16[6144,768]{1,0:T(8,128)(2,1)} custom-call(bf16[192,1536]{1,0:T(8,128)(2,1)} %copy-done.1, bf16[192,1536]{1,0:T(8,128)(2,1)} %collective-permute-done.10.refs_1_, bf16[192,1536]{1,0:T(8,128)(2,1)} %copy-done.12, bf16[192,1536]{1,0:T(8,128)(2,1)} %copy-done.15, ...), custom_call_target="tpu_custom_call", output_to_operand_aliasing={{}: (10, {})} | custom-call | flops 3623878656 | bytes 4718592 | tf_op jit(solution)/shard_map/weight_product/pallas_call | solution.py:105
  (123 shorter events, 24.0 us)
Async XLA Ops:
  9.6 41.4 %collective-permute-start.5 = (bf16[24,6144]{1,0:T(8,128)(2,1)S(1)}, bf16[24,6144]{1,0:T(8,128)(2,1)S(1)}, u32[]{:S(2)}, u32[]{:S(2)}) collective-permute-start(bf16[24,6144]{1,0:T(8,128)(2,1)S(1)} %fusion.26), channel_id=1, source_target_pairs={{0,4},{1,5},{2,6},{3,7},{4,8},{5,9},{6,10},{7,11},{8,12},{9,13},{1... | collective-permute-start | bytes 884744 | tf_op jit(solution)/shard_map/ppermute | solution.py:30
  12.8 38.3 %collective-permute-start.4 = (bf16[24,6144]{1,0:T(8,128)(2,1)S(1)}, bf16[24,6144]{1,0:T(8,128)(2,1)S(1)}, u32[]{:S(2)}, u32[]{:S(2)}) collective-permute-start(bf16[24,6144]{1,0:T(8,128)(2,1)S(1)} %fusion.26), channel_id=1, source_target_pairs={{0,8},{1,9},{2,10},{3,11},{4,12},{5,13},{6,14},{7,15},{8,0},{9,1},... | collective-permute-start | bytes 884744 | tf_op jit(solution)/shard_map/ppermute | solution.py:30
  15.3 35.7 %collective-permute-start.3 = (bf16[24,6144]{1,0:T(8,128)(2,1)S(1)}, bf16[24,6144]{1,0:T(8,128)(2,1)S(1)}, u32[]{:S(2)}, u32[]{:S(2)}) collective-permute-start(bf16[24,6144]{1,0:T(8,128)(2,1)S(1)} %fusion.26), channel_id=1, source_target_pairs={{0,12},{1,13},{2,14},{3,15},{4,0},{5,1},{6,2},{7,3},{8,4},{9,5},{1... | collective-permute-start | bytes 884744 | tf_op jit(solution)/shard_map/ppermute | solution.py:30
  16.7 26.9 %collective-permute-start.2 = (bf16[192,3072]{1,0:T(8,128)(2,1)S(1)}, bf16[192,3072]{1,0:T(8,128)(2,1)S(1)}, u32[]{:S(2)}, u32[]{:S(2)}) collective-permute-start(bf16[192,3072]{1,0:T(8,128)(2,1)S(1)} %fusion.14), channel_id=1, source_target_pairs={{0,2},{1,3},{2,0},{3,1},{4,6},{5,7},{6,4},{7,5},{8,10},{9,11},{10,... | collective-permute-start | bytes 3538952 | tf_op jit(solution)/shard_map/ppermute | solution.py:151
  18.3 3.5 %collective-permute-start = (bf16[384,768]{1,0:T(8,128)(2,1)S(1)}, bf16[384,768]{1,0:T(8,128)(2,1)S(1)}, u32[]{:S(2)}, u32[]{:S(2)}) collective-permute-start(bf16[384,768]{1,0:T(8,128)(2,1)S(1)} %copy-done.20), channel_id=1, source_target_pairs={{0,16},{16,0},{1,17},{17,1},{2,18},{18,2},{3,19},{19,3},{4,20},{20... | collective-permute-start | bytes 1769480 | tf_op jit(solution)/shard_map/ppermute | solution.py:195
  21.7 28.9 %collective-permute-start.1 = (bf16[192,3072]{1,0:T(8,128)(2,1)S(1)}, bf16[192,3072]{1,0:T(8,128)(2,1)S(1)}, u32[]{:S(2)}, u32[]{:S(2)}) collective-permute-start(bf16[192,3072]{1,0:T(8,128)(2,1)S(1)} %fusion.8), channel_id=1, source_target_pairs={{0,1},{1,0},{2,3},{3,2},{4,5},{5,4},{6,7},{7,6},{8,9},{9,8},{10,11... | collective-permute-start | bytes 3538952 | tf_op jit(solution)/shard_map/ppermute | solution.py:151
  44.0 32.7 %collective-permute-start.7 = (bf16[96,3072]{1,0:T(8,128)(2,1)S(1)}, bf16[96,3072]{1,0:T(8,128)(2,1)S(1)}, u32[]{:S(2)}, u32[]{:S(2)}) collective-permute-start(bf16[96,3072]{1,0:T(8,128)(2,1)S(1)} %get-tuple-element.52), channel_id=1, source_target_pairs={{0,1},{1,0},{2,3},{3,2},{4,5},{5,4},{6,7},{7,6},{8,9},{9,8},{10,11... | collective-permute-start | bytes 1769480 | tf_op jit(solution)/shard_map/ppermute | solution.py:151
  51.2 16.3 %collective-permute-start.8 = (bf16[96,3072]{1,0:T(8,128)(2,1)S(1)}, bf16[96,3072]{1,0:T(8,128)(2,1)S(1)}, u32[]{:S(2)}, u32[]{:S(2)}) collective-permute-start(bf16[96,3072]{1,0:T(8,128)(2,1)S(1)} %pad_maximum_fusion.3), channel_id=1, source_target_pairs={{0,2},{1,3},{2,0},{3,1},{4,6},{5,7},{6,4},{7,5},{8,10},{9,11},{10,... | collective-permute-start | bytes 1769480 | tf_op jit(solution)/shard_map/ppermute | solution.py:30
  51.8 23.6 %collective-permute-start.9 = (bf16[96,3072]{1,0:T(8,128)(2,1)S(1)}, bf16[96,3072]{1,0:T(8,128)(2,1)S(1)}, u32[]{:S(2)}, u32[]{:S(2)}) collective-permute-start(bf16[96,3072]{1,0:T(8,128)(2,1)S(1)} %pad_maximum_fusion.4), channel_id=1, source_target_pairs={{0,1},{1,0},{2,3},{3,2},{4,5},{5,4},{6,7},{7,6},{8,9},{9,8},{10,11... | collective-permute-start | bytes 1769480 | tf_op jit(solution)/shard_map/ppermute | solution.py:30
  53.5 25.4 %collective-permute-start.6 = (bf16[96,3072]{1,0:T(8,128)(2,1)S(1)}, bf16[96,3072]{1,0:T(8,128)(2,1)S(1)}, u32[]{:S(2)}, u32[]{:S(2)}) collective-permute-start(bf16[96,3072]{1,0:T(8,128)(2,1)S(1)} %get-tuple-element.55), channel_id=1, source_target_pairs={{0,2},{1,3},{2,0},{3,1},{4,6},{5,7},{6,4},{7,5},{8,10},{9,11},{10,... | collective-permute-start | bytes 1769480 | tf_op jit(solution)/shard_map/ppermute | solution.py:151
  75.6 5.0 %collective-permute-start.19 = (bf16[192,1536]{1,0:T(8,128)(2,1)S(1)}, bf16[192,1536]{1,0:T(8,128)(2,1)S(1)}, u32[]{:S(2)}, u32[]{:S(2)}) collective-permute-start(bf16[192,1536]{1,0:T(8,128)(2,1)S(1)} %pad_maximum_fusion.8.refs_5_), channel_id=1, source_target_pairs={{0,16},{16,0},{1,17},{17,1},{2,18},{18,2},{3,19},{19,3},{4,20},{20... | collective-permute-start | bytes 1769480 | tf_op jit(solution)/shard_map/ppermute | solution.py:242
  75.7 16.3 %collective-permute-start.18 = (bf16[192,1536]{1,0:T(8,128)(2,1)S(1)}, bf16[192,1536]{1,0:T(8,128)(2,1)S(1)}, u32[]{:S(2)}, u32[]{:S(2)}) collective-permute-start(bf16[192,1536]{1,0:T(8,128)(2,1)S(1)} %pad_maximum_fusion.8.refs_5_), channel_id=1, source_target_pairs={{0,2},{1,3},{2,0},{3,1},{4,6},{5,7},{6,4},{7,5},{8,10},{9,11},{10,... | collective-permute-start | bytes 1769480 | tf_op jit(solution)/shard_map/ppermute | solution.py:30
  76.4 18.1 %collective-permute-start.16 = (bf16[192,1536]{1,0:T(8,128)(2,1)S(1)}, bf16[192,1536]{1,0:T(8,128)(2,1)S(1)}, u32[]{:S(2)}, u32[]{:S(2)}) collective-permute-start(bf16[192,1536]{1,0:T(8,128)(2,1)S(1)} %pad_maximum_fusion.7.refs_0_), channel_id=1, source_target_pairs={{0,16},{16,0},{1,17},{17,1},{2,18},{18,2},{3,19},{19,3},{4,20},{20... | collective-permute-start | bytes 1769480 | tf_op jit(solution)/shard_map/ppermute | solution.py:242
  77.3 16.2 %collective-permute-start.15 = (bf16[192,1536]{1,0:T(8,128)(2,1)S(1)}, bf16[192,1536]{1,0:T(8,128)(2,1)S(1)}, u32[]{:S(2)}, u32[]{:S(2)}) collective-permute-start(bf16[192,1536]{1,0:T(8,128)(2,1)S(1)} %pad_maximum_fusion.7.refs_0_), channel_id=1, source_target_pairs={{0,1},{1,0},{2,3},{3,2},{4,5},{5,4},{6,7},{7,6},{8,9},{9,8},{10,11... | collective-permute-start | bytes 1769480 | tf_op jit(solution)/shard_map/ppermute | solution.py:30
  78.9 44.4 %collective-permute-start.11 = (bf16[192,1536]{1,0:T(8,128)(2,1)S(1)}, bf16[192,1536]{1,0:T(8,128)(2,1)}, u32[]{:S(2)}, u32[]{:S(2)}) collective-permute-start(bf16[192,1536]{1,0:T(8,128)(2,1)S(1)} %pad_maximum_fusion.6.refs_5_), channel_id=1, source_target_pairs={{0,2},{1,3},{2,0},{3,1},{4,6},{5,7},{6,4},{7,5},{8,10},{9,11},{10,... | collective-permute-start | bytes 1769480 | tf_op jit(solution)/shard_map/ppermute | solution.py:30
  80.6 42.7 %collective-permute-start.10 = (bf16[192,1536]{1,0:T(8,128)(2,1)S(1)}, bf16[192,1536]{1,0:T(8,128)(2,1)}, u32[]{:S(2)}, u32[]{:S(2)}) collective-permute-start(bf16[192,1536]{1,0:T(8,128)(2,1)S(1)} %pad_maximum_fusion.5.refs_0_), channel_id=1, source_target_pairs={{0,1},{1,0},{2,3},{3,2},{4,5},{5,4},{6,7},{7,6},{8,9},{9,8},{10,11... | collective-permute-start | bytes 1769480 | tf_op jit(solution)/shard_map/ppermute | solution.py:30
  91.9 3.1 %collective-permute-start.20 = (bf16[192,1536]{1,0:T(8,128)(2,1)S(1)}, bf16[192,1536]{1,0:T(8,128)(2,1)S(1)}, u32[]{:S(2)}, u32[]{:S(2)}) collective-permute-start(bf16[192,1536]{1,0:T(8,128)(2,1)S(1)} %collective-permute-done.18.refs_6_), channel_id=1, source_target_pairs={{0,16},{16,0},{1,17},{17,1},{2,18},{18,2},{3,19},{19,3},{4,20},{20... | collective-permute-start | bytes 1769480 | tf_op jit(solution)/shard_map/ppermute | solution.py:242
  93.5 3.4 %collective-permute-start.17 = (bf16[192,1536]{1,0:T(8,128)(2,1)S(1)}, bf16[192,1536]{1,0:T(8,128)(2,1)S(1)}, u32[]{:S(2)}, u32[]{:S(2)}) collective-permute-start(bf16[192,1536]{1,0:T(8,128)(2,1)S(1)} %collective-permute-done.15.refs_1_), channel_id=1, source_target_pairs={{0,16},{16,0},{1,17},{17,1},{2,18},{18,2},{3,19},{19,3},{4,20},{20... | collective-permute-start | bytes 1769480 | tf_op jit(solution)/shard_map/ppermute | solution.py:242
  94.6 15.8 %collective-permute-start.14 = (bf16[24,6144]{1,0:T(8,128)(2,1)}, bf16[24,6144]{1,0:T(8,128)(2,1)S(1)}, u32[]{:S(2)}, u32[]{:S(2)}) collective-permute-start(bf16[24,6144]{1,0:T(8,128)(2,1)} %get-tuple-element.49), channel_id=1, source_target_pairs={{0,12},{1,13},{2,14},{3,15},{4,0},{5,1},{6,2},{7,3},{8,4},{9,5},{1... | collective-permute-start | bytes 884744 | tf_op jit(solution)/shard_map/ppermute | solution.py:151
  95.4 15.6 %collective-permute-start.12 = (bf16[24,6144]{1,0:T(8,128)(2,1)}, bf16[24,6144]{1,0:T(8,128)(2,1)}, u32[]{:S(2)}, u32[]{:S(2)}) collective-permute-start(bf16[24,6144]{1,0:T(8,128)(2,1)} %get-tuple-element.50), channel_id=1, source_target_pairs={{0,4},{1,5},{2,6},{3,7},{4,8},{5,9},{6,10},{7,11},{8,12},{9,13},{1... | collective-permute-start | bytes 884744 | tf_op jit(solution)/shard_map/ppermute | solution.py:151
  97.7 25.6 %collective-permute-start.13 = (bf16[24,6144]{1,0:T(8,128)(2,1)}, bf16[24,6144]{1,0:T(8,128)(2,1)}, u32[]{:S(2)}, u32[]{:S(2)}) collective-permute-start(bf16[24,6144]{1,0:T(8,128)(2,1)} %get-tuple-element.51), channel_id=1, source_target_pairs={{0,8},{1,9},{2,10},{3,11},{4,12},{5,13},{6,14},{7,15},{8,0},{9,1},... | collective-permute-start | bytes 884744 | tf_op jit(solution)/shard_map/ppermute | solution.py:151
  110.3 16.0 %collective-permute-start.23 = (bf16[192,1536]{1,0:T(8,128)(2,1)S(1)}, bf16[192,1536]{1,0:T(8,128)(2,1)S(1)}, u32[]{:S(2)}, u32[]{:S(2)}) collective-permute-start(bf16[192,1536]{1,0:T(8,128)(2,1)S(1)} %pad_maximum_fusion.6.refs_5_), channel_id=1, source_target_pairs={{0,16},{16,0},{1,17},{17,1},{2,18},{18,2},{3,19},{19,3},{4,20},{20... | collective-permute-start | bytes 1769480 | tf_op jit(solution)/shard_map/ppermute | solution.py:242
  111.0 15.3 %collective-permute-start.21 = (bf16[192,1536]{1,0:T(8,128)(2,1)S(1)}, bf16[192,1536]{1,0:T(8,128)(2,1)S(1)}, u32[]{:S(2)}, u32[]{:S(2)}) collective-permute-start(bf16[192,1536]{1,0:T(8,128)(2,1)S(1)} %pad_maximum_fusion.5.refs_0_), channel_id=1, source_target_pairs={{0,16},{16,0},{1,17},{17,1},{2,18},{18,2},{3,19},{19,3},{4,20},{20... | collective-permute-start | bytes 1769480 | tf_op jit(solution)/shard_map/ppermute | solution.py:242
  124.8 3.0 %collective-permute-start.24 = (bf16[192,1536]{1,0:T(8,128)(2,1)}, bf16[192,1536]{1,0:T(8,128)(2,1)S(1)}, u32[]{:S(2)}, u32[]{:S(2)}) collective-permute-start(bf16[192,1536]{1,0:T(8,128)(2,1)} %collective-permute-done.11.refs_6_), channel_id=1, source_target_pairs={{0,16},{16,0},{1,17},{17,1},{2,18},{18,2},{3,19},{19,3},{4,20},{20... | collective-permute-start | bytes 1769480 | tf_op jit(solution)/shard_map/ppermute | solution.py:242
  (26 other events, 153.9 us)
